TPU v7x, 32 devices: a whole 2x2x4 slice. The times are simulated.
32 devices in a mesh: px: 2 (over x), py: 16 (over z, y, core).
Axes of the slice: x: 2, y: 2, z: 4, core: 2. Of those that a mesh axis runs over, the one named last changes fastest.
Arguments:
- populations: float32 [19, 2, 256, 512], P(None, None, ('py', 'px')), may hold values from 0.02 to 0.12
- pore: int32 [2, 256, 512], P(None, ('py', 'px')), may hold values 0 or 1
Outputs:
- flow: float32 [19, 2, 256, 512], P(None, None, 'py', 'px')
All inputs are finite; a program needn't handle non-finite values. No bound on the sum of `pore` on one device may be relied on, other than what follows from the above.
Results may differ from a plain program's by a relative error of at most 0.0001.
Values sent between devices are 32-bit elements; how exact they have to be, the bound alone decides.
A program may use at most 128 MiB of HBM per device.

v0:
```python
import jax
import jax.numpy as jnp
from jax import lax
from jax.sharding import PartitionSpec as P

STEPS = 2
lattice_velocity = [
    (0, 0, 0),
    (1, 0, 0),
    (-1, 0, 0),
    (0, 1, 0),
    (0, -1, 0),
    (0, 0, 1),
    (0, 0, -1),
    (1, 1, 0),
    (-1, -1, 0),
    (1, -1, 0),
    (-1, 1, 0),
    (1, 0, 1),
    (-1, 0, -1),
    (1, 0, -1),
    (-1, 0, 1),
    (0, 1, 1),
    (0, -1, -1),
    (0, 1, -1),
    (0, -1, 1),
]
lattice_weights = [1.0 / 3.0] + [1.0 / 18.0] * 6 + [1.0 / 36.0] * 12
opposite = [0, 2, 1, 4, 3, 6, 5, 8, 7, 10, 9, 12, 11, 14, 13, 16, 15, 18, 17]
relax_time = 0.8
body_force = 0.005


def with_halo(cells, sides, width):
    for axis, dim in sides:
        count = lax.axis_size(axis)
        head = lax.slice_in_dim(cells, 0, width, axis=dim)
        tail = lax.slice_in_dim(cells, cells.shape[dim] - width, cells.shape[dim], axis=dim)
        cells = jnp.concatenate(
            [
                lax.ppermute(tail, axis, [(i, (i + 1) % count) for i in range(count)]),
                cells,
                lax.ppermute(head, axis, [((i + 1) % count, i) for i in range(count)]),
            ],
            axis=dim,
        )
    return cells


def moment(fields, column):
    total = jnp.zeros_like(fields[0])
    for slot in range(len(lattice_velocity)):
        vector = lattice_velocity[slot]
        if vector[column] != 0:
            total = total + float(vector[column]) * fields[slot]
    return total


def collide(fields, fluid):
    density = jnp.where(fluid > 0.5, jnp.sum(fields, axis=0), 1.0)
    vel_first = moment(fields, 0) / density
    vel_second = moment(fields, 1) / density
    vel_third = moment(fields, 2) / density + relax_time * body_force
    speed = vel_first * vel_first + vel_second * vel_second + vel_third * vel_third
    result = []
    for slot in range(len(lattice_velocity)):
        vector = lattice_velocity[slot]
        along = vector[0] * vel_first + vector[1] * vel_second + vector[2] * vel_third
        equil = (
            lattice_weights[slot]
            * density
            * (1.0 + 3.0 * along + 4.5 * along * along - 1.5 * speed)
        )
        result.append(fields[slot] - (fields[slot] - equil) / relax_time)
    return jnp.stack(result) * fluid[None]


def stream(post, fluid):
    height = post.shape[2]
    width = post.shape[3]
    result = []
    for slot in range(len(lattice_velocity)):
        vector = lattice_velocity[slot]
        rows_from = 1 - vector[1]
        cols_from = 1 - vector[0]
        source = post[
            slot, :, rows_from : height - 2 + rows_from, cols_from : width - 2 + cols_from
        ]
        source = jnp.roll(source, vector[2], axis=0)
        open_cell = fluid[:, rows_from : height - 2 + rows_from, cols_from : width - 2 + cols_from]
        open_cell = jnp.roll(open_cell, vector[2], axis=0)
        bounced = post[opposite[slot], :, 1:-1, 1:-1]
        result.append(jnp.where(open_cell > 0.5, source, bounced))
    return jnp.stack(result) * fluid[None, :, 1:-1, 1:-1]


def body(populations, pore):
    count = populations.shape[0]
    stacked = jnp.concatenate([populations, pore.astype(jnp.float32)[None]], axis=0)
    pencil = lax.all_to_all(stacked, "px", split_axis=3, concat_axis=2, tiled=True)
    fields = pencil[:count]
    padded = with_halo(pencil, (("px", 3), ("py", 2)), 2)
    region = padded[count]
    fields = padded[:count]
    for step in range(STEPS):
        post = collide(fields, region)
        fields = stream(post, region)
        region = region[:, 1:-1, 1:-1]
    return fields


def solution(mesh):
    return jax.shard_map(
        body,
        mesh=mesh,
        in_specs=(P(None, None, ("py", "px"), None), P(None, ("py", "px"), None)),
        out_specs=P(None, None, "py", "px"),
        check_vma=False,
    )
```

profile of v0, /device:TPU:0, one launch (start us, length us, event | category | flops | bytes accessed | tf_op | source)
XLA Modules:
  0.0 70.4 jit_solution(6749811037562610711)
XLA Ops:
  0.0 0.8 %convert_bitcast_fusion = f32[1,2,8,512]{3,2,1,0:T(8,128)S(1)} fusion(s32[2,8,512]{2,1,0:T(8,128)} %param.3), kind=kLoop, calls=%fused_computation.539 | loop fusion | flops 8192 | bytes 65536 | tf_op jit(solution)/shard_map/broadcast_in_dim | solution.py:99
  0.8 1.1 %pad_maximum_fusion.1 = f32[20,2,8,512]{3,2,1,0:T(8,128)S(1)} fusion(f32[1,2,8,512]{3,2,1,0:T(8,128)S(1)} %convert_bitcast_fusion, f32[19,2,8,512]{3,2,1,0:T(8,128)} %param.2), kind=kLoop, calls=%fused_computation.5 | loop fusion | flops 163840 | bytes 1310720 | tf_op jit(solution)/shard_map/concatenate | solution.py:99
  1.9 3.8 %copy.6 = f32[20,2,8,512]{0,2,1,3:T(8,128)} copy(f32[20,2,8,512]{3,2,1,0:T(8,128)S(1)} %pad_maximum_fusion.1) | data formatting | bytes 1310720 | tf_op jit(solution)/shard_map/concatenate | solution.py:99
  5.7 6.0 %reshape.453 = f32[2,1,81920]{2,1,0:T(1,128)S(1)} reshape(f32[512,2,8,20]{3,2,1,0:T(8,128)} %bitcast.557) | data formatting | bytes 1310720
  11.7 13.4 %all_to_all.18 = f32[2,1,81920]{2,1,0:T(1,128)S(1)} all-to-all(f32[2,1,81920]{2,1,0:T(1,128)S(1)} %reshape.453), channel_id=1, replica_groups=mesh['px'=2,'py'=16] {'px'}, dimensions={0} | all-to-all | bytes 1310720 | tf_op jit(solution)/shard_map/all_to_all | solution.py:100
  25.1 0.5 broadcast.1003
  25.6 2.7 %reduce = f32[2,81920]{1,0:T(2,128)S(1)} reduce(f32[2,1,81920]{2,1,0:T(1,128)S(1)} %all_to_all.18, f32[]{:T(128)} %broadcast.1003), dimensions={1}, to_apply=%all_to_all.13.reduce_sub_computation | reduce | bytes 1310724 | tf_op jit(solution)/shard_map/all_to_all | solution.py:100
  28.4 6.9 %reshape.454 = f32[512,2,8,20]{3,2,1,0:T(8,128)} reshape(f32[2,81920]{1,0:T(2,128)S(1)} %reduce) | data formatting | bytes 1310720
  35.3 3.0 %copy.7 = f32[20,2,2,8,256]{4,3,2,1,0:T(8,128)S(1)} copy(f32[20,2,2,8,256]{0,3,1,4,2:T(8,128)} %bitcast.558) | data formatting | bytes 1310720 | tf_op jit(solution)/shard_map/all_to_all | solution.py:100
  38.3 0.2 fusion.285
  38.5 0.3 collective-permute-start
  38.8 1.7 %collective-permute-start.1 = (f32[20,2,16,2]{3,2,1,0:T(8,128)S(1)}, f32[20,2,16,2]{3,2,1,0:T(8,128)S(1)}, u32[]{:S(2)}, u32[]{:S(2)}) collective-permute-start(f32[20,2,16,2]{3,2,1,0:T(8,128)S(1)} %get-tuple-element.82), channel_id=1, source_target_pairs={{16,0},{0,16},{17,1},{1,17},{18,2},{2,18},{19,3},{3,19},{20,4},{4,... | collective-permute-start | bytes 15368 | tf_op jit(solution)/shard_map/ppermute | solution.py:43
  40.6 8.6 %collective-permute-done = f32[20,2,16,2]{3,2,1,0:T(8,128)S(1)} collective-permute-done((f32[20,2,16,2]{3,2,1,0:T(8,128)S(1)}, f32[20,2,16,2]{3,2,1,0:T(8,128)S(1)}, u32[]{:S(2)}, u32[]{:S(2)}) %collective-permute-start) | collective-permute-done | bytes 5152 | tf_op jit(solution)/shard_map/ppermute | solution.py:41
  49.1 4.8 %collective-permute-done.1 = f32[20,2,16,2]{3,2,1,0:T(8,128)S(1)} collective-permute-done((f32[20,2,16,2]{3,2,1,0:T(8,128)S(1)}, f32[20,2,16,2]{3,2,1,0:T(8,128)S(1)}, u32[]{:S(2)}, u32[]{:S(2)}) %collective-permute-start.1) | collective-permute-done | bytes 5152 | tf_op jit(solution)/shard_map/ppermute | solution.py:43
  53.9 0.4 pad_maximum_fusion.4
  54.4 4.4 %collective-permute-start.3 = (f32[20,2,2,260]{3,2,1,0:T(2,128)S(1)}, f32[20,2,2,260]{3,2,1,0:T(2,128)S(1)}, u32[]{:S(2)}, u32[]{:S(2)}) collective-permute-start(f32[20,2,2,260]{3,2,1,0:T(2,128)S(1)} %get-tuple-element.80), channel_id=1, source_target_pairs={{1,0},{2,1},{3,2},{4,3},{5,4},{6,5},{7,6},{8,7},{9,8},{10,9},{11,1... | collective-permute-start | bytes 249608 | tf_op jit(solution)/shard_map/ppermute | solution.py:43
  58.8 2.7 %collective-permute-done.2 = f32[20,2,2,260]{3,2,1,0:T(2,128)S(1)} collective-permute-done((f32[20,2,2,260]{3,2,1,0:T(2,128)S(1)}, f32[20,2,2,260]{3,2,1,0:T(2,128)S(1)}, u32[]{:S(2)}, u32[]{:S(2)}) %collective-permute-start.2) | collective-permute-done | bytes 83232 | tf_op jit(solution)/shard_map/ppermute | solution.py:41
  61.5 0.6 pad_maximum_fusion
  62.2 0.2 constant_dynamic-update-slice_fusion.18
  63.3 0.1 broadcast_multiply_fusion.2
  63.5 0.2 fusion.284
  63.8 0.1 slice_bitcast_fusion.37
  64.1 0.1 constant_dynamic-update-slice_fusion.36
  64.2 0.1 constant_dynamic-update-slice_fusion.35
  64.3 0.1 constant_dynamic-update-slice_fusion.34
  64.4 0.1 constant_dynamic-update-slice_fusion.33
  64.6 0.1 constant_dynamic-update-slice_fusion.32
  64.7 0.1 constant_dynamic-update-slice_fusion.31
  64.8 0.1 constant_dynamic-update-slice_fusion.30
  64.9 0.1 constant_dynamic-update-slice_fusion.29
  65.0 0.1 constant_dynamic-update-slice_fusion.28
  65.1 0.1 constant_dynamic-update-slice_fusion.27
  65.2 0.1 constant_dynamic-update-slice_fusion.26
  65.3 0.1 constant_dynamic-update-slice_fusion.25
  65.6 0.1 constant_dynamic-update-slice_fusion.22
  65.7 0.1 constant_dynamic-update-slice_fusion.21
  65.9 0.1 constant_dynamic-update-slice_fusion.19
  66.0 0.1 fusion.282
  66.2 0.2 constant_dynamic-update-slice_fusion.56
  67.3 0.1 broadcast_multiply_fusion
  67.5 0.1 fusion.283
  67.6 0.1 slice_bitcast_fusion.63
  68.0 0.1 constant_dynamic-update-slice_fusion.73
  68.1 0.1 constant_dynamic-update-slice_fusion.72
  68.2 0.1 constant_dynamic-update-slice_fusion.71
  68.6 0.1 constant_dynamic-update-slice_fusion.67
  68.7 0.1 constant_dynamic-update-slice_fusion.65
  69.5 0.9 %broadcast_multiply_fusion.3 = f32[19,2,16,256]{3,2,1,0:T(8,128)} fusion(f32[19,2,16,256]{3,2,1,0:T(8,128)S(1)} %constant_dynamic-update-slice_fusion.57, f32[2,16,256]{2,1,0:T(8,128)S(1)} %slice.1176), kind=kLoop, calls=%fused_computation.6 | loop fusion | flops 155648 | bytes 1277952 | tf_op jit(solution)/shard_map/mul | solution.py:94
  (61 shorter events, 3.8 us)
Async XLA Ops:
  38.5 10.6 %collective-permute-start = (f32[20,2,16,2]{3,2,1,0:T(8,128)S(1)}, f32[20,2,16,2]{3,2,1,0:T(8,128)S(1)}, u32[]{:S(2)}, u32[]{:S(2)}) collective-permute-start(f32[20,2,16,2]{3,2,1,0:T(8,128)S(1)} %get-tuple-element.81), channel_id=1, source_target_pairs={{0,16},{16,0},{1,17},{17,1},{2,18},{18,2},{3,19},{19,3},{4,20},{20... | collective-permute-start | bytes 15368 | tf_op jit(solution)/shard_map/ppermute | solution.py:41
  38.8 15.1 %collective-permute-start.1 = (f32[20,2,16,2]{3,2,1,0:T(8,128)S(1)}, f32[20,2,16,2]{3,2,1,0:T(8,128)S(1)}, u32[]{:S(2)}, u32[]{:S(2)}) collective-permute-start(f32[20,2,16,2]{3,2,1,0:T(8,128)S(1)} %get-tuple-element.82), channel_id=1, source_target_pairs={{16,0},{0,16},{17,1},{1,17},{18,2},{2,18},{19,3},{3,19},{20,4},{4,... | collective-permute-start | bytes 15368 | tf_op jit(solution)/shard_map/ppermute | solution.py:43
  54.3 7.2 %collective-permute-start.2 = (f32[20,2,2,260]{3,2,1,0:T(2,128)S(1)}, f32[20,2,2,260]{3,2,1,0:T(2,128)S(1)}, u32[]{:S(2)}, u32[]{:S(2)}) collective-permute-start(f32[20,2,2,260]{3,2,1,0:T(2,128)S(1)} %get-tuple-element.79), channel_id=1, source_target_pairs={{0,1},{1,2},{2,3},{3,4},{4,5},{5,6},{6,7},{7,8},{8,9},{9,10},{10,1... | collective-permute-start | bytes 249608 | tf_op jit(solution)/shard_map/ppermute | solution.py:41
  54.4 7.1 %collective-permute-start.3 = (f32[20,2,2,260]{3,2,1,0:T(2,128)S(1)}, f32[20,2,2,260]{3,2,1,0:T(2,128)S(1)}, u32[]{:S(2)}, u32[]{:S(2)}) collective-permute-start(f32[20,2,2,260]{3,2,1,0:T(2,128)S(1)} %get-tuple-element.80), channel_id=1, source_target_pairs={{1,0},{2,1},{3,2},{4,3},{5,4},{6,5},{7,6},{8,7},{9,8},{10,9},{11,1... | collective-permute-start | bytes 249608 | tf_op jit(solution)/shard_map/ppermute | solution.py:43
where the time goes:
time: 70.6 us; the launch traced here: 70.4 us
  local copies, waits for them, and re-layouts  21.5 us (30%)
  waiting for transfers between devices  16 us (23%)
  blocking collectives  13.4 us (19%)
  other arithmetic  12.5 us (18%)
  starting transfers between devices  6.58 us (9%)
    all_to_all x1, blocking collectives, body(): lax.all_to_all(stacked, 'px', split_axis=3, concat_axis=2, tiled=True)  13.4 us
    unnamed x4, local copies, waits for them, and re-layouts  13.1 us
    ppermute x2, waiting for transfers between devices, with_halo(): lax.ppermute(tail, axis, [(i, (i + 1) % count) for i in range(count)])  11.2 us
    ppermute x2, starting transfers between devices, with_halo(): lax.ppermute(head, axis, [((i + 1) % count, i) for i in range(count)])  6.17 us
    unnamed x69, other arithmetic  5.24 us
    ppermute x2, waiting for transfers between devices, with_halo(): lax.ppermute(head, axis, [((i + 1) % count, i) for i in range(count)])  4.76 us
    concatenate x1, local copies, waits for them, and re-layouts, body(): jnp.concatenate([populations, pore.astype(jnp.float32)[None]], axis=0)  3.79 us
    all_to_all x2, local copies, waits for them, and re-layouts, body(): lax.all_to_all(stacked, 'px', split_axis=3, concat_axis=2, tiled=True)  3.53 us
  transfers between devices with their start and end apart: 4, of which 3 were waited for; matrix products, arithmetic and copies ran while one was open for 0% of the time, Pallas kernels for 0%

commit v1 on v0

--- a/solution.py
+++ b/solution.py
@@ -2,6 +2,7 @@
 import jax.numpy as jnp
 from jax import lax
 from jax.sharding import PartitionSpec as P
+from jax.lax import all_to_all, axis_size
 
 STEPS = 2
 lattice_velocity = [
@@ -97,7 +98,15 @@
 def body(populations, pore):
     count = populations.shape[0]
     stacked = jnp.concatenate([populations, pore.astype(jnp.float32)[None]], axis=0)
-    pencil = lax.all_to_all(stacked, "px", split_axis=3, concat_axis=2, tiled=True)
+    pencil = jnp.concatenate(
+        all_to_all(
+            jnp.stack(jnp.split(stacked, axis_size("px"), axis=3)),
+            "px",
+            split_axis=0,
+            concat_axis=0,
+        ),
+        axis=2,
+    )
     fields = pencil[:count]
     padded = with_halo(pencil, (("px", 3), ("py", 2)), 2)
     region = padded[count]

time: 70.6 us -> 47.7 us (0.68)
  local copies, waits for them, and re-layouts: 21.5 us -> 1.31 us
  other arithmetic: 12.5 us -> 9.85 us
    unnamed x4 -> x2, local copies, waits for them, and re-layouts: 13.1 us -> 0.16 us
    concatenate x1 -> x0, local copies, waits for them, and re-layouts: 3.79 us -> none  [body(): jnp.concatenate([populations, pore.astype(jnp.float32)[None]], axis=0)]
    all_to_all x2 -> x0, local copies, waits for them, and re-layouts: 3.53 us -> none  [body(): lax.all_to_all(stacked, 'px', split_axis=3, concat_axis=2, tiled=True)]
    all_to_all x1 -> x0, other arithmetic: 2.72 us -> none  [body(): lax.all_to_all(stacked, 'px', split_axis=3, concat_axis=2, tiled=True)]
    another operation x0 -> x2, other arithmetic: none -> 1.15 us  [body(): jnp.stack(jnp.split(stacked, axis_size('px'), axis=3))]
    concatenate x1 -> x0, other arithmetic: 1.13 us -> none  [body(): jnp.concatenate([populations, pore.astype(jnp.float32)[None]], axis=0)]
where the time goes in v1:
time: 47.7 us; the launch traced here: 47.5 us
  waiting for transfers between devices  16 us (34%)
  blocking collectives  13.4 us (28%)
  other arithmetic  9.85 us (21%)
  starting transfers between devices  6.58 us (14%)
  local copies, waits for them, and re-layouts  1.31 us (3%)
    all_to_all x1, blocking collectives, body(): all_to_all(jnp.stack(jnp.split(stacked, axis_size('px'), axis=3)), 'px',...  13.4 us
    ppermute x2, waiting for transfers between devices, with_halo(): lax.ppermute(tail, axis, [(i, (i + 1) % count) for i in range(count)])  11.2 us
    ppermute x2, starting transfers between devices, with_halo(): lax.ppermute(head, axis, [((i + 1) % count, i) for i in range(count)])  6.17 us
    unnamed x69, other arithmetic  5.26 us
    ppermute x2, waiting for transfers between devices, with_halo(): lax.ppermute(head, axis, [((i + 1) % count, i) for i in range(count)])  4.76 us
    another operation x2, other arithmetic, body(): jnp.stack(jnp.split(stacked, axis_size('px'), axis=3))  1.15 us
  transfers between devices with their start and end apart: 4, of which 3 were waited for; matrix products, arithmetic and copies ran while one was open for 0% of the time, Pallas kernels for 0%

profile of v1, /device:TPU:0, one launch (start us, length us, event | category | flops | bytes accessed | tf_op | source)
XLA Modules:
  0.0 47.5 jit_solution(12936284110617349869)
XLA Ops:
  0.0 0.8 %convert_bitcast_fusion = f32[1,2,8,512]{3,2,1,0:T(8,128)S(1)} fusion(s32[2,8,512]{2,1,0:T(8,128)} %param.3), kind=kLoop, calls=%fused_computation.546 | loop fusion | flops 8192 | bytes 65536 | tf_op jit(solution)/shard_map/broadcast_in_dim | solution.py:100
  0.8 1.1 %fusion.1 = (f32[1,20,2,8,256]{4,3,2,1,0:T(8,128)S(1)}, f32[1,20,2,8,256]{4,3,2,1,0:T(8,128)S(1)}) fusion(f32[19,2,8,512]{3,2,1,0:T(8,128)} %param.2, f32[1,2,8,512]{3,2,1,0:T(8,128)S(1)} %convert_bitcast_fusion), kind=kLoop, calls=%fused_computation.10 | loop fusion | flops 163840 | bytes 1310720 | tf_op jit(solution)/shard_map/stack | solution.py:103
  1.9 13.4 %all_to_all.5 = f32[2,20,2,8,256]{4,3,2,1,0:T(8,128)S(1)} all-to-all(f32[2,20,2,8,256]{4,3,2,1,0:T(8,128)S(1)} %pad_maximum_fusion.1), channel_id=1, replica_groups=mesh['px'=2,'py'=16] {'px'}, dimensions={0} | all-to-all | bytes 1310720 | tf_op jit(solution)/shard_map/all_to_all | solution.py:102
  15.4 0.2 fusion.288
  15.6 0.3 collective-permute-start
  15.9 1.7 %collective-permute-start.1 = (f32[20,2,16,2]{3,2,1,0:T(8,128)S(1)}, f32[20,2,16,2]{3,2,1,0:T(8,128)S(1)}, u32[]{:S(2)}, u32[]{:S(2)}) collective-permute-start(f32[20,2,16,2]{3,2,1,0:T(8,128)S(1)} %get-tuple-element.82), channel_id=1, source_target_pairs={{16,0},{0,16},{17,1},{1,17},{18,2},{2,18},{19,3},{3,19},{20,4},{4,... | collective-permute-start | bytes 15368 | tf_op jit(solution)/shard_map/ppermute | solution.py:44
  17.7 8.6 %collective-permute-done = f32[20,2,16,2]{3,2,1,0:T(8,128)S(1)} collective-permute-done((f32[20,2,16,2]{3,2,1,0:T(8,128)S(1)}, f32[20,2,16,2]{3,2,1,0:T(8,128)S(1)}, u32[]{:S(2)}, u32[]{:S(2)}) %collective-permute-start) | collective-permute-done | bytes 5152 | tf_op jit(solution)/shard_map/ppermute | solution.py:42
  26.2 4.8 %collective-permute-done.1 = f32[20,2,16,2]{3,2,1,0:T(8,128)S(1)} collective-permute-done((f32[20,2,16,2]{3,2,1,0:T(8,128)S(1)}, f32[20,2,16,2]{3,2,1,0:T(8,128)S(1)}, u32[]{:S(2)}, u32[]{:S(2)}) %collective-permute-start.1) | collective-permute-done | bytes 5152 | tf_op jit(solution)/shard_map/ppermute | solution.py:44
  31.0 0.4 pad_maximum_fusion.5
  31.5 4.4 %collective-permute-start.3 = (f32[20,2,2,260]{3,2,1,0:T(2,128)S(1)}, f32[20,2,2,260]{3,2,1,0:T(2,128)S(1)}, u32[]{:S(2)}, u32[]{:S(2)}) collective-permute-start(f32[20,2,2,260]{3,2,1,0:T(2,128)S(1)} %get-tuple-element.80), channel_id=1, source_target_pairs={{1,0},{2,1},{3,2},{4,3},{5,4},{6,5},{7,6},{8,7},{9,8},{10,9},{11,1... | collective-permute-start | bytes 249608 | tf_op jit(solution)/shard_map/ppermute | solution.py:44
  35.9 2.7 %collective-permute-done.2 = f32[20,2,2,260]{3,2,1,0:T(2,128)S(1)} collective-permute-done((f32[20,2,2,260]{3,2,1,0:T(2,128)S(1)}, f32[20,2,2,260]{3,2,1,0:T(2,128)S(1)}, u32[]{:S(2)}, u32[]{:S(2)}) %collective-permute-start.2) | collective-permute-done | bytes 83232 | tf_op jit(solution)/shard_map/ppermute | solution.py:42
  38.6 0.6 %pad_maximum_fusion = f32[20,2,20,260]{3,2,1,0:T(8,128)S(1)} fusion(f32[20,2,2,260]{3,2,1,0:T(2,128)S(1)} %collective-permute-done.3, f32[20,2,16,2]{3,2,1,0:T(8,128)S(1)} %collective-permute-done.1, f32[20,2,16,256]{3,2,1,0:T(8,128)S(1)} %copy_bitcast_fusion, f32[20,2,16,2]{3,2,1,0:T(8,128)S(1)} %collective-permute-done, ...), kind=kLoop, calls=%fused_computation | loop fusion | flops 832000 | bytes 1664000 | tf_op jit(solution)/shard_map/concatenate | solution.py:40
  39.3 0.2 constant_dynamic-update-slice_fusion.18
  40.4 0.1 broadcast_multiply_fusion.2
  40.6 0.2 fusion.287
  40.9 0.1 slice_bitcast_fusion.37
  41.2 0.1 constant_dynamic-update-slice_fusion.36
  41.3 0.1 constant_dynamic-update-slice_fusion.35
  41.4 0.1 constant_dynamic-update-slice_fusion.34
  41.5 0.1 constant_dynamic-update-slice_fusion.33
  41.7 0.1 constant_dynamic-update-slice_fusion.32
  41.8 0.1 constant_dynamic-update-slice_fusion.31
  41.9 0.1 constant_dynamic-update-slice_fusion.30
  42.0 0.1 constant_dynamic-update-slice_fusion.29
  42.1 0.1 constant_dynamic-update-slice_fusion.28
  42.2 0.1 constant_dynamic-update-slice_fusion.27
  42.3 0.1 constant_dynamic-update-slice_fusion.26
  42.4 0.1 constant_dynamic-update-slice_fusion.25
  42.5 0.1 constant_dynamic-update-slice_fusion.24
  42.6 0.1 constant_dynamic-update-slice_fusion.23
  42.7 0.1 constant_dynamic-update-slice_fusion.22
  42.8 0.1 constant_dynamic-update-slice_fusion.21
  42.9 0.1 constant_dynamic-update-slice_fusion.20
  43.0 0.1 constant_dynamic-update-slice_fusion.19
  43.1 0.1 fusion.285
  43.3 0.2 constant_dynamic-update-slice_fusion.56
  44.4 0.1 broadcast_multiply_fusion
  44.6 0.1 fusion.286
  44.7 0.1 slice_bitcast_fusion.63
  45.0 0.1 constant_dynamic-update-slice_fusion.74
  45.1 0.1 constant_dynamic-update-slice_fusion.73
  45.2 0.1 constant_dynamic-update-slice_fusion.72
  45.3 0.1 constant_dynamic-update-slice_fusion.71
  45.6 0.1 constant_dynamic-update-slice_fusion.68
  45.7 0.1 constant_dynamic-update-slice_fusion.67
  45.8 0.1 constant_dynamic-update-slice_fusion.66
  45.8 0.1 constant_dynamic-update-slice_fusion.65
  46.6 0.9 %broadcast_multiply_fusion.3 = f32[19,2,16,256]{3,2,1,0:T(8,128)} fusion(f32[19,2,16,256]{3,2,1,0:T(8,128)S(1)} %constant_dynamic-update-slice_fusion.57, f32[2,16,256]{2,1,0:T(8,128)S(1)} %slice.1176), kind=kLoop, calls=%fused_computation.13 | loop fusion | flops 155648 | bytes 1277952 | tf_op jit(solution)/shard_map/mul | solution.py:95
  (57 shorter events, 3.4 us)
Async XLA Ops:
  15.6 10.6 %collective-permute-start = (f32[20,2,16,2]{3,2,1,0:T(8,128)S(1)}, f32[20,2,16,2]{3,2,1,0:T(8,128)S(1)}, u32[]{:S(2)}, u32[]{:S(2)}) collective-permute-start(f32[20,2,16,2]{3,2,1,0:T(8,128)S(1)} %get-tuple-element.81), channel_id=1, source_target_pairs={{0,16},{16,0},{1,17},{17,1},{2,18},{18,2},{3,19},{19,3},{4,20},{20... | collective-permute-start | bytes 15368 | tf_op jit(solution)/shard_map/ppermute | solution.py:42
  15.9 15.1 %collective-permute-start.1 = (f32[20,2,16,2]{3,2,1,0:T(8,128)S(1)}, f32[20,2,16,2]{3,2,1,0:T(8,128)S(1)}, u32[]{:S(2)}, u32[]{:S(2)}) collective-permute-start(f32[20,2,16,2]{3,2,1,0:T(8,128)S(1)} %get-tuple-element.82), channel_id=1, source_target_pairs={{16,0},{0,16},{17,1},{1,17},{18,2},{2,18},{19,3},{3,19},{20,4},{4,... | collective-permute-start | bytes 15368 | tf_op jit(solution)/shard_map/ppermute | solution.py:44
  31.4 7.2 %collective-permute-start.2 = (f32[20,2,2,260]{3,2,1,0:T(2,128)S(1)}, f32[20,2,2,260]{3,2,1,0:T(2,128)S(1)}, u32[]{:S(2)}, u32[]{:S(2)}) collective-permute-start(f32[20,2,2,260]{3,2,1,0:T(2,128)S(1)} %get-tuple-element.79), channel_id=1, source_target_pairs={{0,1},{1,2},{2,3},{3,4},{4,5},{5,6},{6,7},{7,8},{8,9},{9,10},{10,1... | collective-permute-start | bytes 249608 | tf_op jit(solution)/shard_map/ppermute | solution.py:42
  31.5 7.1 %collective-permute-start.3 = (f32[20,2,2,260]{3,2,1,0:T(2,128)S(1)}, f32[20,2,2,260]{3,2,1,0:T(2,128)S(1)}, u32[]{:S(2)}, u32[]{:S(2)}) collective-permute-start(f32[20,2,2,260]{3,2,1,0:T(2,128)S(1)} %get-tuple-element.80), channel_id=1, source_target_pairs={{1,0},{2,1},{3,2},{4,3},{5,4},{6,5},{7,6},{8,7},{9,8},{10,9},{11,1... | collective-permute-start | bytes 249608 | tf_op jit(solution)/shard_map/ppermute | solution.py:44
